TPU v7x, 128 devices: a whole 4x4x4 slice. The times are simulated.
128 devices in a mesh: col: 2 (over core), row: 64 (over z, y, x).
Axes of the slice: x: 4, y: 4, z: 4, core: 2. Of those that a mesh axis runs over, the one named last changes fastest.
Arguments:
- mask: int32 [262144, 1024], P('row', 'col')
- user_emb: bfloat16 [262144, 64], P(('row', 'col'))
- item_emb: bfloat16 [1024, 64], P(('col', 'row'))
- queries: int32 [1024], replicated
Outputs:
- output 1: bfloat16 [262144, 64], P(('row', 'col'))
- output 2: bfloat16 [1024, 64], P(('col', 'row'))
- output 3: float32 [1024, 1024], P(None, ('col', 'row'))
All inputs are finite; a program needn't handle non-finite values.
Results may differ from a plain program's by a relative error of at most 0.00541896.
Values are sent between devices in bfloat16 or wider.
A program may use at most 1 GiB of HBM per device.

v0:
```python
import jax
import jax.numpy as jnp
from jax import lax
from jax.sharding import PartitionSpec as P

LAYERS = 3


def norm_block(mask_blk):
    deg_user = lax.psum(jnp.sum(mask_blk, axis=1), 'col')
    deg_item = lax.psum(jnp.sum(mask_blk, axis=0), 'row')
    inv_user = lax.rsqrt(jnp.maximum(deg_user, 1).astype(jnp.float32))
    inv_item = lax.rsqrt(jnp.maximum(deg_item, 1).astype(jnp.float32))
    return (inv_user[:, None] * mask_blk.astype(jnp.float32) * inv_item[None, :]).astype(jnp.bfloat16)


def query_scores(final_user, final_item, queries, shard_pos):
    rows_local = final_user.shape[0]
    local_idx = queries - shard_pos * rows_local
    owned = (local_idx >= 0) & (local_idx < rows_local)
    picked = jnp.take(final_user, jnp.clip(local_idx, 0, rows_local - 1), axis=0)
    picked = jnp.where(owned[:, None], picked, jnp.zeros_like(picked))
    picked = lax.psum(picked, ('row', 'col'))
    return lax.dot_general(picked, final_item, (((1,), (1,)), ((), ())), preferred_element_type=jnp.float32)


def solution(mesh):
    n_col = mesh.shape['col']
    contract_rows = (((0,), (0,)), ((), ()))

    def device_step(mask_blk, user_shard, item_shard, queries):
        norm_adj = norm_block(mask_blk)
        user_cur = user_shard
        item_cur = item_shard
        user_sum = user_shard.astype(jnp.float32)
        item_sum = item_shard.astype(jnp.float32)
        for layer_idx in range(LAYERS):
            item_panel = lax.all_gather(item_cur, 'row', axis=0, tiled=True)
            user_part = jnp.dot(norm_adj, item_panel, preferred_element_type=jnp.float32)
            user_next = lax.psum_scatter(user_part, 'col', scatter_dimension=0, tiled=True).astype(jnp.bfloat16)
            user_panel = lax.all_gather(user_cur, 'col', axis=0, tiled=True)
            item_part = lax.dot_general(norm_adj, user_panel, contract_rows, preferred_element_type=jnp.float32)
            item_next = lax.psum_scatter(item_part, 'row', scatter_dimension=0, tiled=True).astype(jnp.bfloat16)
            user_sum = user_sum + user_next.astype(jnp.float32)
            item_sum = item_sum + item_next.astype(jnp.float32)
            user_cur = user_next
            item_cur = item_next
        final_user = (user_sum / (LAYERS + 1)).astype(jnp.bfloat16)
        final_item = (item_sum / (LAYERS + 1)).astype(jnp.bfloat16)
        shard_pos = lax.axis_index('row') * n_col + lax.axis_index('col')
        scores = query_scores(final_user, final_item, queries, shard_pos)
        return final_user, final_item, scores

    return jax.shard_map(device_step, mesh=mesh, in_specs=(P('row', 'col'), P(('row', 'col'), None), P(('col', 'row'), None), P()), out_specs=(P(('row', 'col'), None), P(('col', 'row'), None), P(None, ('col', 'row'))), check_vma=False)
```

profile of v0, /device:TPU:1, one launch (start us, length us, event | category | flops | bytes accessed | tf_op | source)
XLA Modules:
  0.0 1451.0 jit_solution(925208205676457116)
XLA Ops:
  7.2 0.0 reduce-scatter.6.cloned.1.call-start
  7.2 0.0 copy-start.3
  7.2 4.1 fusion.1
  11.3 4.5 psum.21
  15.9 20.2 %psum.22 = s32[512]{0:T(512)S(1)} all-reduce(s32[512]{0:T(512)S(1)} %get-tuple-element.4), channel_id=1, replica_groups=mesh['col'=2,'row'=64] {'row'}, use_global_device_ids=true, to_apply=%region_3.0 | all-reduce | flops 512 | bytes 4096 | tf_op jit(solution)/shard_map/psum | solution.py:11
  36.1 0.0 copy-done.3
  36.1 7.2 all_gather.19
  43.3 4.0 multiply_convert_fusion
  47.3 0.0 copy-start
  47.3 1.9 copy-done
  49.3 0.0 copy-start.8
  49.3 1.3 fusion.3
  50.5 286.9 %all-reduce.9 = bf16[512,64]{1,0:T(8,128)(2,1)S(1)} all-reduce(f32[512,64]{1,0:T(8,128)S(1)} %fusion.3), channel_id=3, replica_groups=mesh['col'=2,'row'=64] {'row'}, use_global_device_ids=true, to_apply=%region_5.0.clone | all-reduce | flops 32768 | bytes 196608
  337.5 0.0 copy-done.8
  337.5 0.6 dynamic-slice
  338.7 142.5 %all_gather.20 = bf16[512,64]{1,0:T(8,128)(2,1)S(1)} all-gather(bf16[8,64]{1,0:T(8,128)(2,1)S(1)} %dynamic-slice_convert_fusion.2), channel_id=1, replica_groups=mesh['col'=2,'row'=64] {'row'}, dimensions={0}, use_global_device_ids=true | all-gather | bytes 66560 | tf_op jit(solution)/shard_map/all_gather | solution.py:38
  481.3 0.0 copy-start.6
  481.3 4.6 fusion.4
  485.8 0.0 reduce-scatter.6.cloned.1.call-update
  485.9 0.0 reduce-scatter.4.cloned.1.call-start
  485.9 0.0 copy-done.6
  485.9 143.5 %all_gather.18 = bf16[512,64]{1,0:T(8,128)(2,1)S(1)} all-gather(bf16[8,64]{1,0:T(8,128)(2,1)S(1)} %copy-done.6), channel_id=1, replica_groups=mesh['col'=2,'row'=64] {'row'}, dimensions={0}, use_global_device_ids=true | all-gather | bytes 66560 | tf_op jit(solution)/shard_map/all_gather | solution.py:38
  629.4 4.6 fusion.2
  634.0 0.0 reduce-scatter.4.cloned.1.call-update
  634.1 0.0 reduce-scatter.8.cloned.1.call-start
  634.1 0.0 reduce-scatter.6.cloned.1.call-done
  634.1 1.1 convert_element_type.68
  635.2 113.3 %all_gather.23 = bf16[4096,64]{0,1:T(8,128)(2,1)S(1)} all-gather(bf16[2048,64]{0,1:T(8,128)(2,1)S(1)} %convert_element_type.68), channel_id=1, replica_groups=mesh['col'=2,'row'=64] {'col'}, dimensions={0}, use_global_device_ids=true | all-gather | bytes 786432 | tf_op jit(solution)/shard_map/all_gather | solution.py:41
  748.5 3.5 fusion.7
  752.0 0.0 reduce-scatter.4.cloned.1.call-done
  752.0 1.1 convert_element_type.65
  753.1 2.2 all_gather.21
  755.3 3.5 fusion.5
  758.7 295.8 %all-reduce.10 = (bf16[512,64]{1,0:T(8,128)(2,1)S(1)}, bf16[512,64]{1,0:T(8,128)(2,1)S(1)}) all-reduce(f32[512,64]{1,0:T(8,128)S(1)} %fusion.5, f32[512,64]{1,0:T(8,128)S(1)} %fusion.7), channel_id=5, replica_groups=mesh['col'=2,'row'=64] {'row'}, use_global_device_ids=true, to_apply=%region_7.0.clone | all-reduce | flops 65536 | bytes 393216
  1054.6 0.0 copy-start.7
  1054.6 142.6 %all_gather.22 = bf16[512,64]{1,0:T(8,128)(2,1)S(1)} all-gather(bf16[8,64]{1,0:T(8,128)(2,1)S(1)} %get-tuple-element.8), channel_id=1, replica_groups=mesh['col'=2,'row'=64] {'row'}, dimensions={0}, use_global_device_ids=true | all-gather | bytes 66560 | tf_op jit(solution)/shard_map/all_gather | solution.py:38
  1197.2 0.0 copy-start.5
  1197.2 0.0 copy-start.1
  1197.2 0.0 copy-start.2
  1197.2 4.6 fusion.6
  1201.9 0.0 reduce-scatter.8.cloned.1.call-update
  1201.9 0.0 all-reduce.8.cloned.1.call-start
  1201.9 0.0 copy-done.5
  1202.0 87.4 %reduce-scatter.8.cloned.1.call-done = f32[2048,64]{0,1:T(8,128)} async-done(((f32[4096,64]{0,1:T(8,128)}), f32[2048,64]{0,1:T(8,128)}) %reduce-scatter.8.cloned.1.call-update) | async-done | bytes 524304 | tf_op jit(solution)/shard_map/reduce_scatter | solution.py:40
  1289.4 0.0 copy-done.1
  1289.4 0.0 copy-done.2
  1289.4 1.1 multiply_convert_fusion.1
  1290.5 0.0 copy-start.4
  1290.5 0.3 copy.8
  1290.8 3.2 gather_fusion
  1294.0 1.0 select_select_fusion
  1295.1 0.0 all-reduce.8.cloned.1.call-update
  1295.1 147.7 %all-reduce.8.cloned.1.call-done = bf16[1024,64]{1,0:T(8,128)(2,1)} async-done(((bf16[1024,64]{1,0:T(8,128)(2,1)}), bf16[1024,64]{1,0:T(8,128)(2,1)}) %all-reduce.8.cloned.1.call-update) | async-done | bytes 131088 | tf_op jit(solution)/shard_map/psum | solution.py:23
  1442.7 0.0 copy-done.7
  1442.7 1.7 fusion.8
  1444.5 0.0 copy-done.4
  (6 shorter events, 0.1 us)
Async XLA Ops:
  7.2 627.0 %reduce-scatter.6.cloned.1.call-start = ((), (), s32[]{:S(2)}) async-start(), calls=%async_computation.4 | async-start | bytes 1572864 | tf_op jit(solution)/shard_map/reduce_scatter | solution.py:40
  7.2 28.9 %copy-start.3 = (bf16[2048,64]{0,1:T(8,128)(2,1)S(1)}, bf16[2048,64]{0,1:T(8,128)(2,1)}, u32[]{:S(2)}) copy-start(bf16[2048,64]{0,1:T(8,128)(2,1)} %param.5) | copy-start | bytes 786436
  47.3 1.9 copy-start
  49.3 288.2 %copy-start.8 = (u32[128]{0:T(128)S(1)}, u32[128]{0:T(128)}, u32[]{:S(2)}) copy-start(u32[128]{0:T(128)} %constant.45) | copy-start | bytes 1540
  481.3 4.6 copy-start.6
  485.9 266.1 %reduce-scatter.4.cloned.1.call-start = ((), (), s32[]{:S(2)}) async-start(), calls=%async_computation.3 | async-start | bytes 1572864 | tf_op jit(solution)/shard_map/reduce_scatter | solution.py:40
  634.1 655.3 %reduce-scatter.8.cloned.1.call-start = ((), (), s32[]{:S(2)}) async-start(), calls=%async_computation.5 | async-start | bytes 1572864 | tf_op jit(solution)/shard_map/reduce_scatter | solution.py:40
  1054.6 388.1 %copy-start.7 = (bf16[8,64]{1,0:T(8,128)(2,1)}, bf16[8,64]{1,0:T(8,128)(2,1)S(1)}, u32[]{:S(2)}) copy-start(bf16[8,64]{1,0:T(8,128)(2,1)S(1)} %get-tuple-element.7) | copy-start | bytes 3076
  1197.2 4.7 copy-start.5
  1197.2 92.2 %copy-start.1 = (f32[2048,64]{0,1:T(8,128)S(1)}, f32[2048,64]{0,1:T(8,128)}, u32[]{:S(2)}) copy-start(f32[2048,64]{0,1:T(8,128)} %reduce-scatter.6.cloned.1.call-done) | copy-start | bytes 1572868
  1197.2 92.2 %copy-start.2 = (f32[2048,64]{0,1:T(8,128)S(1)}, f32[2048,64]{0,1:T(8,128)}, u32[]{:S(2)}) copy-start(f32[2048,64]{0,1:T(8,128)} %reduce-scatter.4.cloned.1.call-done) | copy-start | bytes 1572868
  1201.9 240.9 %all-reduce.8.cloned.1.call-start = ((), (), s32[]{:S(2)}) async-start(), calls=%async_computation.6 | async-start | bytes 524288 | tf_op jit(solution)/shard_map/psum | solution.py:23
  1290.5 154.0 %copy-start.4 = (bf16[2048,64]{0,1:T(8,128)(2,1)}, bf16[2048,64]{0,1:T(8,128)(2,1)S(1)}, u32[]{:S(2)}) copy-start(bf16[2048,64]{0,1:T(8,128)(2,1)S(1)} %multiply_convert_fusion.1) | copy-start | bytes 786436
Sparse Core Ops, SparseCore 0:
  486.0 89.0 reduce-scatter.5
  634.2 115.4 reduce-scatter.3
  1202.0 87.3 reduce-scatter.7
  1295.2 147.4 all-reduce.7
where the time goes:
time: 1450 us
  blocking collectives  1160 us (80%)
  waiting for transfers between devices  235 us (16%)
  matrix products  23.8 us (2%)
  between operations  14.6 us (1%)
    unnamed x2, blocking collectives  583 us
    all_gather x3, blocking collectives, device_step(): item_panel = lax.all_gather(item_cur, 'row', axis=0, tiled=True)  429 us
    psum x1, waiting for transfers between devices, query_scores(): picked = lax.psum(picked, ('row', 'col'))  148 us
    all_gather x3, blocking collectives, device_step(): user_panel = lax.all_gather(user_cur, 'col', axis=0, tiled=True)  123 us
    reduce_scatter x3, waiting for transfers between devices, device_step(): lax.psum_scatter(user_part, 'col', scatter_dimension=0, tiled=True)  87.4 us
  transfers between devices with their start and end apart: 4, of which 2 were waited for; matrix products, arithmetic and copies ran while one was open for 1% of the time, Pallas kernels for 0%

commit v1 on v0

v1 whole, which is shorter than its diff:
```python
import jax
import jax.numpy as jnp
from jax import lax
from jax.experimental import pallas as pl
from jax.experimental.pallas import tpu as pltpu
from jax.sharding import PartitionSpec as P

MESH = pl.DeviceIdType.MESH
F32 = jnp.float32
BF16 = jnp.bfloat16
CHUNKS = 8
CHUNK = 512
HALF = 2048
ITEMS = 512
EMB = 64
ROWS = 64
OWN = 8


def peer_row(row, offset):
    peer = row
    for scale in (1, 4, 16):
        digit = (row // scale) % 4
        peer = peer + ((digit + (offset // scale) % 4) % 4 - digit) * scale
    return peer


def step_kernel(mask_hbm, user_ref, item_ref, query_ref, fuser_hbm, fitem_ref, score_ref,
                mask_i, mask_b, mask_o, adj, onehot, deg_src, deg_buf, deg_oth, item_src, item_buf, item0,
                part, pair_buf, red_src, red_buf, gat_src, gat_buf, item12, pick, fuser,
                load_sem, out_sem, send_sem, recv_sem):
    col = lax.axis_index('col')
    row = lax.axis_index('row')
    partner = (1 - col, row)

    loads = []
    for k in range(CHUNKS):
        first = (1 - col) * HALF if k < CHUNKS // 2 else col * HALF - HALF
        start = pl.multiple_of(first + k * CHUNK, CHUNK)
        loads.append(pltpu.make_async_copy(mask_hbm.at[pl.ds(start, CHUNK)], mask_i.at[pl.ds(k * CHUNK, CHUNK)], load_sem.at[k]))
        loads[-1].start()

    barrier = pltpu.get_barrier_semaphore()
    pl.semaphore_signal(barrier, inc=1, device_id=partner, device_id_type=MESH)

    def greet(e, carry):
        pl.semaphore_signal(barrier, inc=1, device_id=(col, peer_row(row, ROWS - e)), device_id_type=MESH)
        return carry
    lax.fori_loop(1, ROWS, greet, 0)

    def send_all(src, dst, sem):
        def one(e, carry):
            pltpu.make_async_remote_copy(src_ref=src, dst_ref=dst.at[row], send_sem=send_sem.at[sem], recv_sem=recv_sem.at[sem],
                                         device_id=(col, peer_row(row, ROWS - e)), device_id_type=MESH).start()
            return carry
        lax.fori_loop(1, ROWS, one, 0)

    def send_chunks(src, dst, sem):
        def one(e, carry):
            back = ROWS - e
            peer = peer_row(row, back)
            pltpu.make_async_remote_copy(src_ref=src.at[pl.ds(pl.multiple_of(peer * OWN, OWN), OWN)], dst_ref=dst.at[back - 1],
                                         send_sem=send_sem.at[sem], recv_sem=recv_sem.at[sem],
                                         device_id=(col, peer), device_id_type=MESH).start()
            return carry
        lax.fori_loop(1, ROWS, one, 0)

    def wait_recv(buf, sem):
        view = buf.at[pl.ds(0, ROWS - 1)]
        pltpu.make_async_copy(view, view, recv_sem.at[sem]).wait()

    def wait_sent(buf, sem):
        view = buf.at[pl.ds(0, ROWS - 1)]
        pltpu.make_async_copy(view, view, send_sem.at[sem]).wait()

    def to_partner(src, dst, sem):
        copy = pltpu.make_async_remote_copy(src_ref=src, dst_ref=dst, send_sem=send_sem.at[sem], recv_sem=recv_sem.at[sem],
                                            device_id=partner, device_id_type=MESH)
        copy.start()
        return copy

    own_item = item_ref[...].astype(F32)
    item_src[...] = jnp.concatenate([own_item, own_item], axis=1)

    count = jnp.zeros((8, ITEMS), jnp.int32)
    for k in range(CHUNKS):
        loads[k].wait()
        block = mask_i[pl.ds(k * CHUNK, CHUNK), :]
        count = count + jnp.sum(block.reshape(CHUNK // 8, 8, ITEMS), axis=0)
        mask_b[pl.ds(k * CHUNK, CHUNK), :] = block.astype(F32).astype(BF16)
    deg_own = jnp.sum(count, axis=0, keepdims=True)
    deg_src[...] = deg_own

    pl.semaphore_wait(barrier, ROWS)
    send_all(deg_src, deg_buf, 0)
    mask_copy = to_partner(mask_b.at[pl.ds(0, HALF)], mask_o, 1)
    send_all(item_src, item_buf, 2)

    query = query_ref[...]
    low, high = query[:, :ITEMS], query[:, ITEMS:]
    ordered = jnp.concatenate([jnp.where(col == 0, low, high), jnp.where(col == 0, high, low)], axis=1)
    local = ordered - (row * 2 + col) * HALF
    spread = jnp.transpose(jnp.broadcast_to(local, (128, 2 * ITEMS)))
    lane = lax.broadcasted_iota(jnp.int32, (2 * ITEMS, 128), 1)
    for k in range(HALF // 128):
        onehot[:, pl.ds(k * 128, 128)] = jnp.where(spread == lane + k * 128, 1.0, 0.0).astype(BF16)

    mask_copy.wait()
    ones = jnp.ones((ITEMS, 128), BF16)
    deg_user = (jnp.dot(mask_b[pl.ds(HALF, HALF), :], ones, preferred_element_type=F32)
                + jnp.dot(mask_o[...], ones, preferred_element_type=F32))
    inv_user = lax.rsqrt(jnp.maximum(deg_user, 1.0))

    wait_recv(item_buf, 2)
    item_buf[row] = item_src[...]
    item0[0] = item_buf[...].reshape(ITEMS, 128).astype(BF16)
    item_copy = to_partner(item0.at[0], item0.at[1], 3)

    wait_recv(deg_buf, 0)
    deg_buf[row] = deg_src[...]
    deg_item = jnp.sum(deg_buf[...], axis=0)
    wait_sent(deg_buf, 0)
    deg_src[...] = deg_item
    deg_copy = to_partner(deg_src, deg_oth, 4)

    def form(item_degree, mask_block, half):
        inv_item = lax.rsqrt(jnp.maximum(item_degree, 1).astype(F32))
        for k in range(ITEMS // 128):
            scale = (inv_user * inv_item[:, k * 128:(k + 1) * 128]).astype(BF16)
            adj[:, pl.ds(half * ITEMS + k * 128, 128)] = scale * mask_block[:, k * 128:(k + 1) * 128]

    form(deg_item, mask_b[pl.ds(HALF, HALF), :], 0)
    deg_copy.wait()
    form(deg_oth[...], mask_o[...], 1)
    item_copy.wait()

    user0 = user_ref[...]
    user1 = jnp.dot(adj[...], item0[...].reshape(2 * ITEMS, 128), preferred_element_type=F32).astype(BF16)
    user01 = jnp.concatenate([user0, user1[:, EMB:]], axis=1)

    def reduce_items(index):
        to_partner(part.at[pl.ds(ITEMS, ITEMS)], pair_buf.at[index], 5 + 4 * index).wait()
        red_src[index] = part[pl.ds(0, ITEMS), :] + pair_buf[index]
        send_chunks(red_src.at[index], red_buf.at[index], 6 + 4 * index)
        wait_recv(red_buf.at[index], 6 + 4 * index)
        total = red_src[index, pl.ds(pl.multiple_of(row * OWN, OWN), OWN), :] + jnp.sum(red_buf[index], axis=0)
        return total

    part[...] = jnp.transpose(jnp.dot(jnp.transpose(user01), adj[...], preferred_element_type=F32))
    own12 = reduce_items(0).astype(BF16).astype(F32)
    gat_src[0] = own12
    send_all(gat_src.at[0], gat_buf.at[0], 7)
    item_sum = (own_item + own12[:, :EMB]) + own12[:, EMB:]
    wait_recv(gat_buf.at[0], 7)
    gat_buf[0, row] = own12
    item12[0] = gat_buf[0].reshape(ITEMS, 128).astype(BF16)
    to_partner(item12.at[0], item12.at[1], 8).wait()

    user23 = jnp.dot(adj[...], item12[...].reshape(2 * ITEMS, 128), preferred_element_type=F32).astype(BF16)
    item3 = jnp.transpose(jnp.dot(jnp.transpose(user23[:, :EMB]), adj[...], preferred_element_type=F32))
    user_sum = ((user0.astype(F32) + user1[:, :EMB].astype(F32)) + user23[:, :EMB].astype(F32)) + user23[:, EMB:].astype(F32)
    final = (user_sum / 4.0).astype(BF16)
    fuser[...] = final
    out_copy = pltpu.make_async_copy(fuser, fuser_hbm, out_sem.at[0])
    out_copy.start()
    picked = jnp.dot(onehot[...], jnp.concatenate([final, final], axis=1), preferred_element_type=F32)
    part[...] = jnp.concatenate([item3, picked[:, EMB:]], axis=1)
    own3 = reduce_items(1)
    gat_src[1] = own3
    send_all(gat_src.at[1], gat_buf.at[1], 11)
    final_item = ((item_sum + own3[:, :EMB].astype(BF16).astype(F32)) / 4.0).astype(BF16)
    fitem_ref[...] = final_item
    weights = jnp.concatenate([jnp.zeros((OWN, EMB), BF16), final_item], axis=1)
    wait_recv(gat_buf.at[1], 11)
    gat_buf[1, row] = own3
    pick[0] = gat_buf[1].reshape(ITEMS, 128).astype(BF16)
    pick_copy = to_partner(pick.at[0], pick.at[1], 12)
    contract = (((1,), (1,)), ((), ()))
    score_ref[pl.ds(pl.multiple_of(col * ITEMS, ITEMS), ITEMS), :] = lax.dot_general(pick[0], weights, contract, preferred_element_type=F32)
    pick_copy.wait()
    score_ref[pl.ds(pl.multiple_of((1 - col) * ITEMS, ITEMS), ITEMS), :] = lax.dot_general(pick[1], weights, contract, preferred_element_type=F32)

    out_copy.wait()
    wait_sent(item_buf, 2)
    wait_sent(red_buf.at[0], 6)
    wait_sent(red_buf.at[1], 10)
    wait_sent(gat_buf.at[0], 7)
    wait_sent(gat_buf.at[1], 11)


def solution(mesh):
    vmem = pl.BlockSpec(memory_space=pltpu.VMEM)
    hbm = pl.BlockSpec(memory_space=pl.ANY)

    def device_step(mask_blk, user_shard, item_shard, queries):
        return pl.pallas_call(
            step_kernel,
            out_shape=(jax.ShapeDtypeStruct((HALF, EMB), BF16), jax.ShapeDtypeStruct((OWN, EMB), BF16),
                       jax.ShapeDtypeStruct((2 * ITEMS, OWN), F32)),
            in_specs=[hbm, vmem, vmem, vmem],
            out_specs=(hbm, vmem, vmem),
            scratch_shapes=[
                pltpu.VMEM((2 * HALF, ITEMS), jnp.int32),
                pltpu.VMEM((2 * HALF, ITEMS), BF16),
                pltpu.VMEM((HALF, ITEMS), BF16),
                pltpu.VMEM((HALF, 2 * ITEMS), BF16),
                pltpu.VMEM((2 * ITEMS, HALF), BF16),
                pltpu.VMEM((1, ITEMS), jnp.int32),
                pltpu.VMEM((ROWS, 1, ITEMS), jnp.int32),
                pltpu.VMEM((1, ITEMS), jnp.int32),
                pltpu.VMEM((OWN, 128), F32),
                pltpu.VMEM((ROWS, OWN, 128), F32),
                pltpu.VMEM((2, ITEMS, 128), BF16),
                pltpu.VMEM((2 * ITEMS, 128), F32),
                pltpu.VMEM((2, ITEMS, 128), F32),
                pltpu.VMEM((2, ITEMS, 128), F32),
                pltpu.VMEM((2, ROWS - 1, OWN, 128), F32),
                pltpu.VMEM((2, OWN, 128), F32),
                pltpu.VMEM((2, ROWS, OWN, 128), F32),
                pltpu.VMEM((2, ITEMS, 128), BF16),
                pltpu.VMEM((2, ITEMS, 128), BF16),
                pltpu.VMEM((HALF, EMB), BF16),
                pltpu.SemaphoreType.DMA((CHUNKS,)),
                pltpu.SemaphoreType.DMA((1,)),
                pltpu.SemaphoreType.DMA((13,)),
                pltpu.SemaphoreType.DMA((13,)),
            ],
            compiler_params=pltpu.CompilerParams(collective_id=0, has_side_effects=True, vmem_limit_bytes=60 * 1024 * 1024),
        )(mask_blk, user_shard, item_shard, queries.reshape(1, 2 * ITEMS))

    return jax.shard_map(device_step, mesh=mesh, in_specs=(P('row', 'col'), P(('row', 'col'), None), P(('col', 'row'), None), P()),
                         out_specs=(P(('row', 'col'), None), P(('col', 'row'), None), P(None, ('col', 'row'))), check_vma=False)
```

time: 1450 us -> 72.4 us (0.05)
  blocking collectives: 1160 us -> 0 us
  waiting for transfers between devices: 235 us -> 0 us
  Pallas kernels: 0 us -> 64.5 us
  matrix products: 23.8 us -> 0 us
    unnamed x2 -> x0, blocking collectives: 583 us -> none
    all_gather x6 -> x0, blocking collectives: 551 us -> none  [the longest x3 429 us: device_step(): item_panel = lax.all_gather(item_cur, 'row', axis=0, tiled=True)]
    psum x1 -> x0, waiting for transfers between devices: 148 us -> none  [query_scores(): picked = lax.psum(picked, ('row', 'col'))]
    reduce_scatter x3 -> x0, waiting for transfers between devices: 87.4 us -> none  [device_step(): lax.psum_scatter(user_part, 'col', scatter_dimension=0, tiled=True)]
    pallas_call x0 -> x1, Pallas kernels: none -> 64.5 us  [device_step(): pl.pallas_call(step_kernel, out_shape=(jax.ShapeDtypeStruct((HALF, EMB),...]
    psum x2 -> x0, blocking collectives: 24.8 us -> none  [the longest x1 20.2 us: norm_block(): deg_item = lax.psum(jnp.sum(mask_blk, axis=0), 'row')]
    dot_general x7 -> x0, matrix products: 23.8 us -> none  [the longest x3 13.8 us: device_step(): jnp.dot(norm_adj, item_panel, preferred_element_type=jnp.float32)]
  transfers between devices with their start and end apart: 4 -> 0, of which waited for: 2 -> 0; matrix products, arithmetic and copies ran while one was open for 1% -> 0% of each run, Pallas kernels for 0% -> 0%
where the time goes in v1:
time: 72.4 us; the launch traced here: 72.1 us
  Pallas kernels  64.5 us (89%)
  local copies, waits for them, and re-layouts  6.95 us (10%)
    pallas_call x1, Pallas kernels, device_step(): pl.pallas_call(step_kernel, out_shape=(jax.ShapeDtypeStruct((HALF, EMB),...  64.5 us
    pallas_call x2, local copies, waits for them, and re-layouts, device_step(): pl.pallas_call(step_kernel, out_shape=(jax.ShapeDtypeStruct((HALF, EMB),...  3.76 us
    unnamed x2, local copies, waits for them, and re-layouts  3.19 us

profile of v1, /device:TPU:1, one launch (start us, length us, event | category | flops | bytes accessed | tf_op | source)
XLA Modules:
  0.0 72.1 jit_solution(16516352431397418547)
XLA Ops:
  0.6 1.9 %copy.7.user_ref = bf16[2048,64]{1,0:T(8,128)(2,1)} copy(bf16[2048,64]{0,1:T(8,128)(2,1)} %param.5) | data formatting | bytes 524288 | tf_op args[1]
  2.6 64.5 %shard_map.67 = (bf16[2048,64]{1,0:T(8,128)(2,1)}, bf16[8,64]{1,0:T(8,128)(2,1)}, f32[1024,8]{1,0:T(8,128)}) custom-call(s32[4096,512]{1,0:T(8,128)} %mask_hbm.1, bf16[2048,64]{1,0:T(8,128)(2,1)} %copy.7.user_ref, bf16[8,64]{1,0:T(8,128)(2,1)} %item_ref.1, s32[1,1024]{1,0:T(1,128)} %bitcast.1), custom_call_target="tpu_custom_call" | custom-call | tf_op jit(solution)/shard_map/pallas_call | solution.py:196
  67.1 1.9 %copy.8 = bf16[2048,64]{0,1:T(8,128)(2,1)} copy(bf16[2048,64]{1,0:T(8,128)(2,1)} %get-tuple-element.3) | data formatting | bytes 524288 | tf_op jit(solution)/shard_map/pallas_call | solution.py:196
  69.1 1.8 %copy.9 = f32[1024,8]{0,1:T(8,128)} copy(f32[1024,8]{1,0:T(8,128)} %get-tuple-element.5) | data formatting | bytes 65536 | tf_op jit(solution)/shard_map/pallas_call | solution.py:196
  70.9 1.2 %copy.11 = bf16[8,64]{1,0:T(8,128)(2,1)} copy(bf16[8,64]{1,0:T(8,128)(2,1)} %get-tuple-element.10) | data formatting | bytes 2048

commit v2 on v0

v2 whole, which is shorter than its diff:
```python
import jax
import jax.numpy as jnp
from jax import lax
from jax.experimental import pallas as pl
from jax.experimental.pallas import tpu as pltpu
from jax.sharding import PartitionSpec as P

MESH = pl.DeviceIdType.MESH
F32 = jnp.float32
BF16 = jnp.bfloat16
CHUNKS = 8
CHUNK = 512
HALF = 2048
ITEMS = 512
ALL_ITEMS = 1024
EMB = 64
ROWS = 64
OWN = 8
HOPS = (0, 1, 2, 1)
LAST = (((1,), (1,)), ((), ()))

PLACES = [(p, z, y, x) for p in range(2) for z in range(4) for y in range(4) for x in range(4)][1:]
PLACES.sort(key=lambda place: (-sum(HOPS[d] for d in place[1:]), place))
SAME_CORE = [place for place in PLACES if place[0] == 0]
LINE_X = [(0, 0, 0, d) for d in (2, 1, 3)]
LINE_Y = [(0, 0, d, 0) for d in (2, 1, 3)]
LINE_Z = [(p, d, 0, 0) for d in (2, 1, 3, 0) for p in (1, 0) if p or d]


def step_kernel(mask_hbm, user_hbm, item_hbm, query_hbm, fuser_out, fitem_out, score_out,
                mask_i, mask_b, mask_o, adj, onehot, inv_user, user01, item_own, query, deg_src, deg_x, deg_y, deg_z,
                item_src, item_pair, item_quad, item_x, item_y, item_z,
                part, pair_buf, red_src, red_buf, gat_src, gat_buf, pick_src, pick_buf, fuser, fitem, score,
                load_sem, in_sem, out_sem, send_sem, recv_sem):
    col = lax.axis_index('col')
    row = lax.axis_index('row')
    at_x, at_y, at_z = row % 4, (row // 4) % 4, row // 16
    xs = [(at_x + d) % 4 for d in range(4)]
    ys = [((at_y + d) % 4) * 4 for d in range(4)]
    zs = [((at_z + d) % 4) * 16 for d in range(4)]
    cols = [col, 1 - col]
    partner = (1 - col, row)

    def device(place):
        p, z, y, x = place
        return cols[p], zs[z] + ys[y] + xs[x]

    loads = []
    for k in range(CHUNKS):
        first = (1 - col) * HALF if k < CHUNKS // 2 else col * HALF - HALF
        start = pl.multiple_of(first + k * CHUNK, CHUNK)
        loads.append(pltpu.make_async_copy(mask_hbm.at[pl.ds(start, CHUNK)], mask_i.at[pl.ds(k * CHUNK, CHUNK)], load_sem.at[k]))
        loads[-1].start()
    small = [pltpu.make_async_copy(item_hbm, item_own, in_sem.at[0]), pltpu.make_async_copy(query_hbm, query, in_sem.at[1]),
             pltpu.make_async_copy(user_hbm, user01.at[pl.ds(0, EMB)], in_sem.at[2])]
    for copy in small:
        copy.start()

    with jax.named_scope('greet'):
        barrier = pltpu.get_barrier_semaphore()
        for place in LINE_X + LINE_Y + LINE_Z:
            pl.semaphore_signal(barrier, inc=1, device_id=device(place), device_id_type=MESH)

    def send_to(places, src, dst, sem):
        for place in places:
            pltpu.make_async_remote_copy(src_ref=src, dst_ref=dst, send_sem=send_sem.at[sem], recv_sem=recv_sem.at[sem],
                                         device_id=device(place), device_id_type=MESH).start()

    def send_chunks(src, dst, sem):
        for n, place in enumerate(SAME_CORE):
            target = device(place)
            rows = pl.ds(pl.multiple_of(target[1] * OWN, OWN), OWN)
            pltpu.make_async_remote_copy(src_ref=src.at[rows], dst_ref=dst.at[n], send_sem=send_sem.at[sem], recv_sem=recv_sem.at[sem],
                                         device_id=target, device_id_type=MESH).start()

    def wait_slots(buf, sem, slots):
        view = buf.at[pl.ds(0, slots)]
        pltpu.make_async_copy(view, view, sem).wait()

    def to_partner(src, dst, sem):
        copy = pltpu.make_async_remote_copy(src_ref=src, dst_ref=dst, send_sem=send_sem.at[sem], recv_sem=recv_sem.at[sem],
                                            device_id=partner, device_id_type=MESH)
        copy.start()
        return copy

    with jax.named_scope('load'):
        small[0].wait()
        own_item = item_own[...]
        item_src[...] = jnp.concatenate([own_item, own_item], axis=1)
        count = jnp.zeros((8, ITEMS), jnp.int32)
        for k in range(CHUNKS):
            loads[k].wait()
            block = mask_i[pl.ds(k * CHUNK, CHUNK), :]
            count = count + jnp.sum(block.reshape(CHUNK // 8, 8, ITEMS), axis=0)
            mask_b[pl.ds(k * CHUNK, CHUNK), :] = block.astype(F32).astype(BF16)
        deg_src[0] = jnp.sum(count, axis=0, keepdims=True)
    with jax.named_scope('barrier'):
        pl.semaphore_wait(barrier, len(LINE_X + LINE_Y + LINE_Z))

    lower = lax.broadcasted_iota(jnp.int32, (OWN, 128), 1) < EMB
    with jax.named_scope('send_x'):
        send_to(LINE_X, deg_src.at[0], deg_x.at[at_x], 0)
        send_to(LINE_X, item_src, item_x.at[at_x], 2)
        mask_copy = to_partner(mask_b.at[pl.ds(0, HALF)], mask_o, 1)

    with jax.named_scope('onehot'):
        small[1].wait()
        ids = query[...]
        low, high = ids[:, :ITEMS], ids[:, ITEMS:]
        ordered = jnp.concatenate([jnp.where(col == 0, low, high), jnp.where(col == 0, high, low)], axis=1)
        local = jnp.broadcast_to(ordered - (row * 2 + col) * HALF, (128, ALL_ITEMS))
        place_in = lax.broadcasted_iota(jnp.int32, (128, ALL_ITEMS), 0)
        for k in range(HALF // 128):
            onehot[pl.ds(k * 128, 128), :] = jnp.where(local == place_in + k * 128, 1.0, 0.0).astype(BF16)

    with jax.named_scope('wait_x'):
        wait_slots(deg_x, recv_sem.at[0], 3)
        deg_x[at_x] = deg_src[0]
        deg_src[1] = jnp.sum(deg_x[...], axis=0)
        send_to(LINE_Y, deg_src.at[1], deg_y.at[at_y], 9)
    with jax.named_scope('wait_x2'):
        wait_slots(item_x, recv_sem.at[2], 3)
        item_x[at_x] = item_src[...]
        for n in range(2):
            item_pair[n] = jnp.where(lower, item_x[2 * n].astype(F32), item_x[2 * n + 1].astype(F32)).astype(BF16)
        send_to(LINE_Y, item_pair, item_y.at[at_y], 10)

    with jax.named_scope('mask_wait'):
        mask_copy.wait()
    with jax.named_scope('deg_user'):
        ones = jnp.ones((ITEMS, 128), BF16)
        deg_user = (jnp.dot(mask_b[pl.ds(HALF, HALF), :], ones, preferred_element_type=F32)
                    + jnp.dot(mask_o[...], ones, preferred_element_type=F32))
        inv_user[...] = lax.rsqrt(jnp.maximum(deg_user, 1.0))

    with jax.named_scope('wait_y'):
        wait_slots(deg_y, recv_sem.at[9], 3)
        deg_y[at_y] = deg_src[1]
        deg_src[2] = jnp.sum(deg_y[...], axis=0)
        send_to(LINE_Z, deg_src.at[2], deg_z.at[col * 4 + at_z], 11)
    with jax.named_scope('wait_y2'):
        wait_slots(item_y, recv_sem.at[10], 3)
        item_y[at_y] = item_pair[...]
        item_quad[...] = item_y[...]
        send_to(LINE_Z, item_quad, item_z.at[col * 4 + at_z], 12)
        small[2].wait()

    def own_first(buf):
        return jnp.where(col == 0, buf[0], buf[1]), jnp.where(col == 0, buf[1], buf[0])

    with jax.named_scope('wait_z'):
        wait_slots(deg_z, recv_sem.at[11], 7)
        deg_z[col * 4 + at_z] = deg_src[2]
        deg_all = own_first(jnp.sum(deg_z[...].reshape(2, 4, 1, ITEMS), axis=1))
        inv_item = [lax.rsqrt(jnp.maximum(deg, 1).astype(F32)) for deg in deg_all]

    def form(chunk):
        for half in range(2):
            rows = pl.ds(chunk * CHUNK, CHUNK)
            block = mask_b[pl.ds(HALF + chunk * CHUNK, CHUNK), :] if half == 0 else mask_o[rows, :]
            for k in range(ITEMS // 128):
                scale = (inv_user[rows, :] * inv_item[half][:, k * 128:(k + 1) * 128]).astype(BF16)
                adj[rows, pl.ds(half * ITEMS + k * 128, 128)] = scale * block[:, k * 128:(k + 1) * 128]

    with jax.named_scope('form0'):
        form(0)
    with jax.named_scope('wait_item0'):
        wait_slots(item_z, recv_sem.at[12], 7)
        item_z[col * 4 + at_z] = item_quad[...]
        packed = item_z[...].astype(F32)
        turned = pltpu.roll(packed.reshape(64 * OWN, 128), EMB, 1).reshape(packed.shape)
        rows = jnp.stack([packed, turned], axis=3).reshape(2, ITEMS, 128)
        item0 = jnp.concatenate([jnp.transpose(half)[:EMB] for half in own_first(rows)], axis=1).astype(BF16)
    with jax.named_scope('m1'):
        for k in range(HALF // CHUNK):
            if k:
                form(k)
            user1 = lax.dot_general(item0, adj[pl.ds(k * CHUNK, CHUNK), :], LAST, preferred_element_type=F32).astype(BF16)
            user01[pl.ds(EMB, EMB), pl.ds(k * CHUNK, CHUNK)] = user1

    def reduce_items(index, make):
        with jax.named_scope('make%d' % index):
            part[1] = make(1)
            copy = to_partner(part.at[1], pair_buf.at[index], 3 + 3 * index)
            part[0] = make(0)
        with jax.named_scope('pair%d' % index):
            copy.wait()
            red_src[index] = part[0] + pair_buf[index]
        with jax.named_scope('send_red%d' % index):
            send_chunks(red_src.at[index], red_buf.at[index], 4 + 3 * index)

    def reduced(index):
        with jax.named_scope('wait_red%d' % index):
            wait_slots(red_buf.at[index], recv_sem.at[4 + 3 * index], ROWS - 1)
        return red_src[index, pl.ds(pl.multiple_of(row * OWN, OWN), OWN), :] + jnp.sum(red_buf[index], axis=0)

    reduce_items(0, lambda half: jnp.transpose(jnp.dot(user01[...], adj[:, half * ITEMS:(half + 1) * ITEMS], preferred_element_type=F32)))
    own12 = reduced(0).astype(BF16)
    with jax.named_scope('send_gat'):
        gat_src[...] = own12
        send_to(PLACES, gat_src, gat_buf.at[col * ROWS + row], 5)
    item_sum = (own_item.astype(F32) + own12[:, :EMB].astype(F32)) + own12[:, EMB:].astype(F32)
    with jax.named_scope('wait_gat'):
        wait_slots(gat_buf, recv_sem.at[5], 2 * ROWS - 1)
        gat_buf[col * ROWS + row] = own12
    with jax.named_scope('t12'):
        rows = gat_buf[...].astype(F32).reshape(2, ITEMS, 128)
        item12 = jnp.concatenate([jnp.transpose(half) for half in own_first(rows)], axis=1).astype(BF16)
    with jax.named_scope('m3'):
        user23 = lax.dot_general(item12, adj[...], LAST, preferred_element_type=F32).astype(BF16)
        user_sum = (user01[:EMB, :].astype(F32) + user01[EMB:, :].astype(F32)) + user23[:EMB].astype(F32)
        final = ((user_sum + user23[EMB:].astype(F32)) / 4.0).astype(BF16)
        fuser[...] = final
    out_copy = pltpu.make_async_copy(fuser, fuser_out, out_sem.at[0])
    out_copy.start()

    def item3_and_picks(half):
        cut = slice(half * ITEMS, (half + 1) * ITEMS)
        item3 = jnp.dot(user23[:EMB], adj[:, cut], preferred_element_type=F32)
        picked = jnp.dot(final, onehot[:, cut], preferred_element_type=F32)
        return jnp.transpose(jnp.concatenate([item3, picked], axis=0))

    reduce_items(1, item3_and_picks)
    own3 = reduced(1)
    with jax.named_scope('send_pick'):
        pick_src[...] = own3.astype(BF16)
        send_to(PLACES, pick_src, pick_buf.at[col * ROWS + row], 8)
    final_item = ((item_sum + own3[:, :EMB].astype(BF16).astype(F32)) / 4.0).astype(BF16)
    fitem[...] = final_item
    weights = jnp.concatenate([jnp.zeros((OWN, EMB), BF16), final_item], axis=1)
    with jax.named_scope('wait_pick'):
        wait_slots(pick_buf, recv_sem.at[8], 2 * ROWS - 1)
        pick_buf[col * ROWS + row] = pick_src[...]
    with jax.named_scope('score'):
        rows = pick_buf[...].astype(F32).reshape(ALL_ITEMS, 128).astype(BF16)
        score[...] = lax.dot_general(weights, rows, LAST, preferred_element_type=F32)
    with jax.named_scope('finish'):
        outs = [pltpu.make_async_copy(fitem, fitem_out, out_sem.at[1]), pltpu.make_async_copy(score, score_out, out_sem.at[2])]
        for copy in outs:
            copy.start()
        for buf, sem, slots in ((deg_x, 0, 3), (deg_y, 9, 3), (deg_z, 11, 7), (item_x, 2, 3), (item_y, 10, 3), (item_z, 12, 7),
                                (red_buf.at[0], 4, ROWS - 1), (gat_buf, 5, 2 * ROWS - 1), (red_buf.at[1], 7, ROWS - 1),
                                (pick_buf, 8, 2 * ROWS - 1)):
            wait_slots(buf, send_sem.at[sem], slots)
        out_copy.wait()
        for copy in outs:
            copy.wait()


def hand_over(fuser_in, fitem_in, score_in, fuser_out, fitem_out, score_out):
    fuser_out[...] = fuser_in[...]
    fitem_out[...] = fitem_in[...]
    score_out[...] = score_in[...]


def solution(mesh):
    hbm = pl.BlockSpec(memory_space=pl.ANY)
    vmem = pl.BlockSpec(memory_space=pltpu.VMEM)
    shapes = (jax.ShapeDtypeStruct((EMB, HALF), BF16), jax.ShapeDtypeStruct((OWN, EMB), BF16), jax.ShapeDtypeStruct((OWN, ALL_ITEMS), F32))

    def device_step(mask_blk, user_shard, item_shard, queries):
        outs = pl.pallas_call(
            step_kernel,
            out_shape=shapes,
            in_specs=[hbm, hbm, hbm, hbm],
            out_specs=(hbm, hbm, hbm),
            scratch_shapes=[
                pltpu.VMEM((2 * HALF, ITEMS), jnp.int32),
                pltpu.VMEM((2 * HALF, ITEMS), BF16),
                pltpu.VMEM((HALF, ITEMS), BF16),
                pltpu.VMEM((HALF, ALL_ITEMS), BF16),
                pltpu.VMEM((HALF, ALL_ITEMS), BF16),
                pltpu.VMEM((HALF, 128), F32),
                pltpu.VMEM((2 * EMB, HALF), BF16),
                pltpu.VMEM((OWN, EMB), BF16),
                pltpu.VMEM((1, ALL_ITEMS), jnp.int32),
                pltpu.VMEM((3, 1, ITEMS), jnp.int32),
                pltpu.VMEM((4, 1, ITEMS), jnp.int32),
                pltpu.VMEM((4, 1, ITEMS), jnp.int32),
                pltpu.VMEM((8, 1, ITEMS), jnp.int32),
                pltpu.VMEM((OWN, 128), BF16),
                pltpu.VMEM((2, OWN, 128), BF16),
                pltpu.VMEM((4, 2, OWN, 128), BF16),
                pltpu.VMEM((4, OWN, 128), BF16),
                pltpu.VMEM((4, 2, OWN, 128), BF16),
                pltpu.VMEM((8, 4, 2, OWN, 128), BF16),
                pltpu.VMEM((2, ITEMS, 128), F32),
                pltpu.VMEM((2, ITEMS, 128), F32),
                pltpu.VMEM((2, ITEMS, 128), F32),
                pltpu.VMEM((2, ROWS - 1, OWN, 128), F32),
                pltpu.VMEM((OWN, 128), BF16),
                pltpu.VMEM((2 * ROWS, OWN, 128), BF16),
                pltpu.VMEM((OWN, 128), BF16),
                pltpu.VMEM((2 * ROWS, OWN, 128), BF16),
                pltpu.VMEM((EMB, HALF), BF16),
                pltpu.VMEM((OWN, EMB), BF16),
                pltpu.VMEM((OWN, ALL_ITEMS), F32),
                pltpu.SemaphoreType.DMA((CHUNKS,)),
                pltpu.SemaphoreType.DMA((3,)),
                pltpu.SemaphoreType.DMA((3,)),
                pltpu.SemaphoreType.DMA((13,)),
                pltpu.SemaphoreType.DMA((13,)),
            ],
            compiler_params=pltpu.CompilerParams(collective_id=0, has_side_effects=True, vmem_limit_bytes=60 * 1024 * 1024),
        )(mask_blk, user_shard.T, item_shard, queries.reshape(1, ALL_ITEMS))
        fuser, fitem, score = pl.pallas_call(hand_over, out_shape=shapes, in_specs=[vmem] * 3, out_specs=(vmem,) * 3)(*outs)
        return fuser.T, fitem, score.T

    return jax.shard_map(device_step, mesh=mesh, in_specs=(P('row', 'col'), P(('row', 'col'), None), P(('col', 'row'), None), P()),
                         out_specs=(P(('row', 'col'), None), P(('col', 'row'), None), P(None, ('col', 'row'))), check_vma=False)
```

time: 1450 us -> 58.8 us (0.04)
  blocking collectives: 1160 us -> 0 us
  waiting for transfers between devices: 235 us -> 0 us
  Pallas kernels: 0 us -> 58.1 us
  matrix products: 23.8 us -> 0 us
    unnamed x2 -> x0, blocking collectives: 583 us -> none
    all_gather x6 -> x0, blocking collectives: 551 us -> none  [the longest x3 429 us: device_step(): item_panel = lax.all_gather(item_cur, 'row', axis=0, tiled=True)]
    psum x1 -> x0, waiting for transfers between devices: 148 us -> none  [query_scores(): picked = lax.psum(picked, ('row', 'col'))]
    reduce_scatter x3 -> x0, waiting for transfers between devices: 87.4 us -> none  [device_step(): lax.psum_scatter(user_part, 'col', scatter_dimension=0, tiled=True)]
    pallas_call x0 -> x2, Pallas kernels: none -> 58.1 us  [the longest x1 56.4 us: device_step(): pl.pallas_call(step_kernel, out_shape=shapes, in_specs=[hbm, hbm, hbm, hb...]
    psum x2 -> x0, blocking collectives: 24.8 us -> none  [the longest x1 20.2 us: norm_block(): deg_item = lax.psum(jnp.sum(mask_blk, axis=0), 'row')]
    dot_general x7 -> x0, matrix products: 23.8 us -> none  [the longest x3 13.8 us: device_step(): jnp.dot(norm_adj, item_panel, preferred_element_type=jnp.float32)]
  transfers between devices with their start and end apart: 4 -> 0, of which waited for: 2 -> 0; matrix products, arithmetic and copies ran while one was open for 1% -> 0% of each run, Pallas kernels for 0% -> 0%
where the time goes in v2:
time: 58.8 us; the launch traced here: 58.7 us
  Pallas kernels  58.1 us (99%)
  between operations  0.64 us (1%)
    pallas_call x1, Pallas kernels, device_step(): pl.pallas_call(step_kernel, out_shape=shapes, in_specs=[hbm, hbm, hbm, hb...  56.4 us
    pallas_call x1, Pallas kernels, device_step(): pl.pallas_call(hand_over, out_shape=shapes, in_specs=[vmem] * 3, out_spec...  1.68 us

profile of v2, /device:TPU:1, one launch (start us, length us, event | category | flops | bytes accessed | tf_op | source)
XLA Modules:
  0.0 58.7 jit_solution(14424173207023470712)
XLA Ops:
  0.6 56.4 %shard_map.67 = (bf16[64,2048]{1,0:T(8,128)(2,1)}, bf16[8,64]{1,0:T(8,128)(2,1)}, f32[8,1024]{1,0:T(8,128)}) custom-call(s32[4096,512]{1,0:T(8,128)} %mask_hbm.1, bf16[64,2048]{1,0:T(8,128)(2,1)} %bitcast.4, bf16[8,64]{1,0:T(8,128)(2,1)} %item_hbm.1, s32[1,1024]{1,0:T(1,128)} %bitcast.5), custom_call_target="tpu_custom_call" | custom-call | tf_op jit(solution)/shard_map/pallas_call | solution.py:262
  57.0 1.7 %shard_map.68 = (bf16[64,2048]{1,0:T(8,128)(2,1)}, bf16[8,64]{1,0:T(8,128)(2,1)}, f32[8,1024]{1,0:T(8,128)}) custom-call(bf16[64,2048]{1,0:T(8,128)(2,1)} %get-tuple-element.9.fuser_in, bf16[8,64]{1,0:T(8,128)(2,1)} %get-tuple-element.10.fitem_in, f32[8,1024]{1,0:T(8,128)} %get-tuple-element.11.score_in), custom_call_target="tpu_custom_call" | custom-call | tf_op jit(solution)/shard_map/pallas_call | solution.py:306
